TPU v7x, 256 devices: a whole 4x4x8 slice. The times are simulated.
256 devices in a mesh: gx: 32 (over x, z), gy: 8 (over y, core).
Axes of the slice: x: 4, y: 4, z: 8, core: 2. Of those that a mesh axis runs over, the one named last changes fastest.
Arguments:
- parcel_props: float32 [16, 1048576], P(None, ('gx', 'gy')), may hold values from -6 to 6
- size_class: int32 [1048576], P(('gx', 'gy')), may hold values from 0 to 7
- dest_owner: int32 [1048576, 1], P(('gx', 'gy')), may hold values from 0 to 255; in each aligned block of 4096 rows (0 to 4095, 4096 to 8191, ...) at most 64 rows name the same one
- dest_local: int32 [1048576], P(('gx', 'gy')), may hold values from 0 to 4095
- class_table: float32 [8, 16], replicated, may hold values from 0.5 to 2
- gas_density: float32 [1024, 1024], P('gx', 'gy'), may hold values from 0.5 to 2
- gas_rest: float32 [4, 1024, 1024], P(None, 'gx', 'gy'), may hold values from -6 to 6
Outputs:
- new_density: float32 [1024, 1024], P('gx', 'gy')
- new_rest: float32 [4, 1024, 1024], P(None, 'gx', 'gy')
Inputs may be any that keep to these rules, and one draw needn't show every extreme that they name: `dest_owner`: among the parcels of one device, no owner device is named by more than 64 of them, a bound that some block reaches.
All inputs are finite; a program needn't handle non-finite values.
Results may differ from a plain program's by a relative error of at most 0.00015.
Values sent between devices are 32-bit elements; how exact they have to be, the bound alone decides.
A program may use at most 64 MiB of HBM per device.

v0:
```python
import functools

import jax
import jax.numpy as jnp
from jax import lax
from jax.experimental import pallas as pl
from jax.experimental.pallas import tpu as pltpu
from jax.sharding import PartitionSpec as P

MESH = pl.DeviceIdType.MESH
F32 = jnp.float32
BF16 = jnp.bfloat16

X, Z, Y, CORES = 4, 8, 4, 2
DEVICES = X * Z * Y * CORES
PARCELS = 4096
CAP = 64
LX, LY = 32, 128
WORDS = 8
STEP = 256
GROUPS = 8
GROUP = DEVICES // GROUPS


def offsets():
    far = [
        (dx, dz, dy, dc)
        for dy in range(Y)
        for dc in range(CORES)
        for dx in range(X)
        for dz in (4, 1, 7, 2, 6, 3, 5, 0)
        if dx or dz or dy or dc
    ]
    return [(0, 0, 0, 0)] + far


def here():
    gx = lax.axis_index("gx")
    gy = lax.axis_index("gy")
    return gx // Z, gx % Z, gy // CORES, gy % CORES


def peer(at, dx, dz, dy, dc):
    x, z, y, core = at
    return (((x + dx) % X) * Z + (z + dz) % Z, ((y + dy) % Y) * CORES + (core + dc) % CORES)


def signal(sem, to):
    pl.semaphore_signal(sem, inc=1, device_id=to, device_id_type=MESH)


def in_row(at):
    return [peer(at, 0, 0, dy, dc) for dy in range(Y) for dc in range(CORES) if dy or dc]


def in_column(at):
    return [peer(at, dx, dz, 0, 0) for dx in range(X) for dz in range(Z) if dx or dz]


def two_parts(v):
    high = v.astype(BF16).astype(F32)
    return high, v - high


def iota(shape, dim):
    return lax.broadcasted_iota(jnp.int32, shape, dim)


def wide_row(ref, step):
    return jnp.concatenate([ref[2 * step : 2 * step + 1], ref[2 * step + 1 : 2 * step + 2]], axis=1)


def spread(row, height):
    part = jnp.broadcast_to(row, (16, row.shape[1])).astype(BF16)
    return jnp.concatenate([part] * (height // 16), axis=0)


def dot_last(a, b):
    return lax.dot_general(a, b, (((1,), (1,)), ((), ())), preferred_element_type=F32)


def pack(props, classes, owners, locals_, table, blocks, packed):
    across = iota((STEP, STEP), 1)
    down = iota((STEP, STEP), 0)
    earlier = (down < across).astype(F32).astype(BF16)
    ones = jnp.ones((STEP, 128), BF16)
    carry = jnp.zeros((DEVICES, 128), F32)
    columns = jnp.transpose(jnp.concatenate([table[...], jnp.zeros((8, 112), F32)], axis=1))[:16]
    columns = [jnp.broadcast_to(columns[:, k : k + 1], (16, STEP)) for k in range(8)]
    for step in range(PARCELS // STEP):
        owner = wide_row(owners, step)
        mine = down == owner
        member = jnp.where(mine, 1.0, 0.0).astype(BF16)
        before = jnp.dot(member, earlier, preferred_element_type=F32)
        before = before + jnp.concatenate([carry, carry], axis=1)
        rank = jnp.sum(jnp.where(mine, before, 0.0), axis=0, keepdims=True)
        carry = carry + jnp.dot(member, ones, preferred_element_type=F32)

        q = props[:, step * STEP : (step + 1) * STEP]
        kind = wide_row(classes, step)
        coef = columns[0]
        for k in range(1, 8):
            coef = jnp.where(kind == k, columns[k], coef)
        made = jnp.where(iota((16, STEP), 0) >= 5, coef * q, 0.0)
        energy = q[4:5] + jnp.sum(made, axis=0, keepdims=True)
        local = wide_row(locals_, step).astype(F32)
        words = [q[0:1], q[1:2], q[2:3], q[3:4], q[4:5], energy, kind.astype(F32) + 1.0, local]

        hot = jnp.where(iota((CAP, STEP), 0).astype(F32) == rank, 1.0, 0.0).astype(BF16)
        parts = [two_parts(w) for w in words]
        held = [hot * spread(p[0], CAP) for p in parts] + [hot * spread(p[1], CAP) for p in parts]
        placed = dot_last(jnp.concatenate(held, axis=0), member)
        placed = placed[: WORDS * CAP] + placed[WORDS * CAP :]
        if step:
            packed[...] += placed
        else:
            packed[...] = placed
    for j in range(WORDS // 2):
        blocks[:, j, :] = jnp.transpose(packed[128 * j : 128 * j + 128, :])


def look_up(gas_rows, hi, lo):
    found = [jnp.zeros(hi.shape, F32) for _ in range(5)]
    for h in range(LX):
        at = hi == h
        for k in range(5):
            row = jnp.broadcast_to(gas_rows(k, h), hi.shape)
            found[k] = jnp.where(at, jnp.take_along_axis(row, lo, axis=1, mode="promise_in_bounds"), found[k])
    return found


def sources(words, gas, table):
    q0, q1, q2, q3, q4, energy, kind, _ = words
    coef = []
    for j in range(5):
        c = jnp.full(q0.shape, table[0, j], F32)
        for k in range(1, 8):
            c = jnp.where(kind == k + 1.0, table[k, j], c)
        coef.append(c)
    mass = jnp.where(kind > 0.5, jnp.exp(0.5 * q0), 0.0)
    inverse = 1.0 / gas[0]
    slip = [q - m * inverse for q, m in zip((q1, q2, q3), gas[1:4])]
    warm = q4 - gas[4] * inverse
    rate = coef[0] * (jnp.maximum(warm, 0.0) + jnp.log1p(jnp.exp(-jnp.abs(warm))))
    evapor = mass * (1.0 - jnp.exp(-rate))
    speed = 1.0 + slip[0] * slip[0] + slip[1] * slip[1] + slip[2] * slip[2]
    dragged = mass * (1.0 - jnp.exp(-coef[1] * jnp.sqrt(speed)))
    moment = [evapor * c * q + dragged * w for c, q, w in zip(coef[2:5], (q1, q2, q3), slip)]
    return [evapor, *moment, evapor * energy]


def receive_group(group, recv, gas_rows, table, dense, deposit):
    lane = iota((8, 128), 1)
    for half in range(GROUP // 16):
        first = group * GROUP + 16 * half
        words = []
        for j in range(WORDS // 2):
            a = recv[first : first + 8, j, :]
            b = recv[first + 8 : first + 16, j, :]
            words.append(jnp.where(lane < 64, a, pltpu.roll(b, 64, 1)))
            words.append(jnp.where(lane < 64, pltpu.roll(a, 64, 1), b))
        cell = words[7].astype(jnp.int32)
        hi, lo = cell >> 7, cell & 127
        src = sources(words, look_up(gas_rows, hi, lo), table)
        rows = slice(8 * half, 8 * half + 8)
        for k in range(5):
            dense[2 * k, rows], dense[2 * k + 1, rows] = two_parts(src[k])
        dense[10, rows] = hi.astype(F32)
        dense[11, rows] = lo.astype(F32)
    total = jnp.zeros((320, LY), F32)
    for step in range(GROUP * CAP // STEP):
        at_hi = jnp.where(iota((LX, STEP), 0).astype(F32) == wide_row(dense.at[10], step), 1.0, 0.0).astype(BF16)
        at_lo = jnp.where(iota((LY, STEP), 0).astype(F32) == wide_row(dense.at[11], step), 1.0, 0.0).astype(BF16)
        held = [at_hi * spread(wide_row(dense.at[2 * k + p], step), LX) for p in (0, 1) for k in range(5)]
        total = total + dot_last(jnp.concatenate(held, axis=0), at_lo)
    total = total[:160] + total[160:]
    if group:
        deposit[...] += total
    else:
        deposit[...] = total


def kernel(
    props, classes, owners, locals_, table, table_s, density, rest,
    new_density, new_rest,
    blocks, packed, recv, dense, deposit, edges, halo,
    second, send_sem, recv_sem, edge_sem, halo_sem,
):
    at = here()
    gx, gy = lax.axis_index("gx"), lax.axis_index("gy")
    barrier = pltpu.get_barrier_semaphore()
    row, column = in_row(at), in_column(at)
    for to in row + column:
        signal(barrier, to)

    pack(props, classes, owners, locals_, table, blocks, packed)

    pl.semaphore_wait(barrier, len(row) + len(column))
    for to in row:
        signal(second, to)
    pl.semaphore_wait(second, len(row))

    order = offsets()
    for slot, off in enumerate(order):
        if slot:
            to = peer(at, *off)
            pltpu.make_async_remote_copy(
                src_ref=blocks.at[to[0] * 8 + to[1]],
                dst_ref=recv.at[slot],
                send_sem=send_sem,
                recv_sem=recv_sem.at[slot // GROUP],
                device_id=to,
                device_id_type=MESH,
            ).start()
    recv[0] = blocks[gx * 8 + gy]

    def gas_rows(k, h):
        return density[h : h + 1] if k == 0 else rest[k - 1, h : h + 1]

    def arrived(copies, sem):
        pltpu.make_async_copy(blocks.at[:copies], recv.at[:copies], sem).wait()

    for group in range(GROUPS):
        arrived(GROUP if group else GROUP - 1, recv_sem.at[group])
        receive_group(group, recv, gas_rows, table_s, dense, deposit)
    arrived(DEVICES - 1, send_sem)

    lane = iota((8, 128), 1)
    low_column = jnp.zeros((8, 128), F32)
    high_column = jnp.zeros((8, 128), F32)
    for i in range(20):
        tile = deposit[8 * i : 8 * i + 8]
        low_column = jnp.where(lane == i, pltpu.roll(tile, i, 1) if i else tile, low_column)
        high_column = jnp.where(lane == i, pltpu.roll(tile, i + 1, 1), high_column)
    pad = jnp.zeros((3, 128), F32)
    edges[0] = jnp.concatenate([deposit[32 * k : 32 * k + 1] for k in range(5)] + [pad], axis=0)
    edges[1] = jnp.concatenate([deposit[32 * k + 31 : 32 * k + 32] for k in range(5)] + [pad], axis=0)
    edges[2] = low_column
    edges[3] = high_column
    beside = [
        ((gx + 31) % 32, gy),
        ((gx + 1) % 32, gy),
        (gx, (gy + 7) % 8),
        (gx, (gy + 1) % 8),
    ]
    copies = [
        pltpu.make_async_remote_copy(
            src_ref=edges.at[i],
            dst_ref=halo.at[i],
            send_sem=edge_sem.at[i],
            recv_sem=halo_sem.at[i],
            device_id=to,
            device_id_type=MESH,
        )
        for i, to in enumerate(beside)
    ]
    for copy in copies:
        copy.start()
    for copy in copies:
        copy.wait()

    def kept(value, there):
        return jnp.where(there, value, 0.0)

    above = kept(halo[0], gx < 31)
    below = kept(halo[1], gx > 0)
    right = kept(halo[2], gy < 7)
    left = kept(halo[3], gy > 0)
    for k in range(5):
        field = deposit[32 * k : 32 * k + 32]
        up = jnp.concatenate([field[1:], above[k : k + 1]], axis=0)
        down = jnp.concatenate([below[k : k + 1], field[:-1]], axis=0)
        rights, lefts = [], []
        for i in range(4 * k, 4 * k + 4):
            tile = deposit[8 * i : 8 * i + 8]
            rights.append(jnp.where(lane == 127, pltpu.roll(right, 127 - i, 1), pltpu.roll(tile, 127, 1)))
            lefts.append(jnp.where(lane == 0, pltpu.roll(left, 128 - i, 1) if i else left, pltpu.roll(tile, 1, 1)))
        around = up + down + jnp.concatenate(rights, axis=0) + jnp.concatenate(lefts, axis=0)
        smooth = 0.4 * field + 0.15 * around
        if k == 0:
            new_density[...] = density[...] + smooth
        else:
            new_rest[k - 1] = rest[k - 1] + smooth


def per_device(parcel_props, size_class, dest_owner, dest_local, class_table, gas_density, gas_rest):
    vmem = pl.BlockSpec(memory_space=pltpu.VMEM)
    smem = pl.BlockSpec(memory_space=pltpu.SMEM)
    return pl.pallas_call(
        kernel,
        out_shape=(
            jax.ShapeDtypeStruct((LX, LY), F32),
            jax.ShapeDtypeStruct((4, LX, LY), F32),
        ),
        in_specs=[vmem, vmem, vmem, vmem, vmem, smem, vmem, vmem],
        out_specs=(vmem, vmem),
        scratch_shapes=[
            pltpu.VMEM((DEVICES, WORDS // 2, 128), F32),
            pltpu.VMEM((WORDS * CAP, DEVICES), F32),
            pltpu.VMEM((DEVICES, WORDS // 2, 128), F32),
            pltpu.VMEM((12, GROUP // 2, 128), F32),
            pltpu.VMEM((160, LY), F32),
            pltpu.VMEM((4, 8, 128), F32),
            pltpu.VMEM((4, 8, 128), F32),
            pltpu.SemaphoreType.REGULAR,
            pltpu.SemaphoreType.DMA,
            pltpu.SemaphoreType.DMA((GROUPS,)),
            pltpu.SemaphoreType.DMA((4,)),
            pltpu.SemaphoreType.DMA((4,)),
        ],
        compiler_params=pltpu.CompilerParams(collective_id=0, has_side_effects=True),
    )(
        parcel_props,
        size_class.reshape(32, 128),
        dest_owner.reshape(32, 128),
        dest_local.reshape(32, 128),
        class_table,
        class_table,
        gas_density,
        gas_rest,
    )


def solution(mesh):
    return jax.shard_map(
        per_device,
        mesh=mesh,
        in_specs=(
            P(None, ("gx", "gy")),
            P(("gx", "gy")),
            P(("gx", "gy"), None),
            P(("gx", "gy")),
            P(),
            P("gx", "gy"),
            P(None, "gx", "gy"),
        ),
        out_specs=(P("gx", "gy"), P(None, "gx", "gy")),
        check_vma=False,
    )
```

profile of v0, /device:TPU:1, one launch (start us, length us, event | category | flops | bytes accessed | tf_op | source)
XLA Modules:
  0.0 40.8 jit_solution(8006914966588512159)
XLA Ops:
  0.6 37.4 %shard_map.86 = (f32[32,128]{1,0:T(8,128)}, f32[4,32,128]{2,1,0:T(8,128)}) custom-call(f32[16,4096]{1,0:T(8,128)} %props.1, s32[32,128]{1,0:T(8,128)} %bitcast.3, s32[32,128]{1,0:T(8,128)} %bitcast.4, s32[32,128]{1,0:T(8,128)} %bitcast.5, f32[8,16]{1,0:T(8,128)} %table_s.1, f32[8,16]{1,0:T(8,128)} %table_s.1, f32[32,128]{1,0:T(8,128)} %density.1, ...), custom_call_target="tpu_custom_call" | custom-call | tf_op jit(solution)/shard_map/pallas_call | solution.py:289
  38.0 1.3 %copy.11 = f32[32,128]{1,0:T(8,128)} copy(f32[32,128]{1,0:T(8,128)} %get-tuple-element.4) | data formatting | bytes 32768
  39.4 1.5 %copy.12 = f32[4,32,128]{2,1,0:T(8,128)} copy(f32[4,32,128]{2,1,0:T(8,128)} %get-tuple-element.5) | data formatting | bytes 131072
where the time goes:
time: 41 us; the launch traced here: 40.8 us
  Pallas kernels  37.4 us (91%)
  local copies, waits for them, and re-layouts  2.8 us (7%)
  between operations  0.64 us (2%)
    pallas_call x1, Pallas kernels, per_device(): pl.pallas_call(kernel, out_shape=(jax.ShapeDtypeStruct((LX, LY), F32), ja...  37.4 us
    unnamed x2, local copies, waits for them, and re-layouts  2.8 us

commit v1 on v0

--- a/solution.py
+++ b/solution.py
@@ -1,5 +1,3 @@
-import functools
-
 import jax
 import jax.numpy as jnp
 from jax import lax
@@ -22,16 +20,12 @@
 GROUP = DEVICES // GROUPS
 
 
+PLANES = (0, 1, 7, 2, 6, 3, 5, 4)
+
+
 def offsets():
-    far = [
-        (dx, dz, dy, dc)
-        for dy in range(Y)
-        for dc in range(CORES)
-        for dx in range(X)
-        for dz in (4, 1, 7, 2, 6, 3, 5, 0)
-        if dx or dz or dy or dc
-    ]
-    return [(0, 0, 0, 0)] + far
+    flat = [(dx, dy, dc) for dx in range(X) for dy in range(Y) for dc in range(CORES)]
+    return [(dx, dz, dy, dc) for dz in PLANES for dx, dy, dc in flat]
 
 
 def here():
@@ -49,12 +43,9 @@
     pl.semaphore_signal(sem, inc=1, device_id=to, device_id_type=MESH)
 
 
-def in_row(at):
-    return [peer(at, 0, 0, dy, dc) for dy in range(Y) for dc in range(CORES) if dy or dc]
-
-
-def in_column(at):
-    return [peer(at, dx, dz, 0, 0) for dx in range(X) for dz in range(Z) if dx or dz]
+def in_plane(at):
+    flat = [(dx, dy, dc) for dx in range(X) for dy in range(Y) for dc in range(CORES)]
+    return [peer(at, dx, 0, dy, dc) for dx, dy, dc in flat if dx or dy or dc]
 
 
 def two_parts(v):
@@ -79,7 +70,7 @@
     return lax.dot_general(a, b, (((1,), (1,)), ((), ())), preferred_element_type=F32)
 
 
-def pack(props, classes, owners, locals_, table, blocks, packed):
+def pack(props, classes, owners, locals_, table, blocks, packed, midway):
     across = iota((STEP, STEP), 1)
     down = iota((STEP, STEP), 0)
     earlier = (down < across).astype(F32).astype(BF16)
@@ -88,6 +79,8 @@
     columns = jnp.transpose(jnp.concatenate([table[...], jnp.zeros((8, 112), F32)], axis=1))[:16]
     columns = [jnp.broadcast_to(columns[:, k : k + 1], (16, STEP)) for k in range(8)]
     for step in range(PARCELS // STEP):
+        if step == 10:
+            midway()
         owner = wide_row(owners, step)
         mine = down == owner
         member = jnp.where(mine, 1.0, 0.0).astype(BF16)
@@ -149,7 +142,7 @@
     return [evapor, *moment, evapor * energy]
 
 
-def receive_group(group, recv, gas_rows, table, dense, deposit):
+def find_sources(group, recv, gas_rows, table, dense):
     lane = iota((8, 128), 1)
     for half in range(GROUP // 16):
         first = group * GROUP + 16 * half
@@ -167,6 +160,9 @@
             dense[2 * k, rows], dense[2 * k + 1, rows] = two_parts(src[k])
         dense[10, rows] = hi.astype(F32)
         dense[11, rows] = lo.astype(F32)
+
+
+def add_sources(group, dense, deposit):
     total = jnp.zeros((320, LY), F32)
     for step in range(GROUP * CAP // STEP):
         at_hi = jnp.where(iota((LX, STEP), 0).astype(F32) == wide_row(dense.at[10], step), 1.0, 0.0).astype(BF16)
@@ -181,29 +177,44 @@
 
 
 def kernel(
-    props, classes, owners, locals_, table, table_s, density, rest,
-    new_density, new_rest,
-    blocks, packed, recv, dense, deposit, edges, halo,
-    second, send_sem, recv_sem, edge_sem, halo_sem,
+    props_h, classes_h, owners_h, locals_h, table, table_s, density_h, rest_h,
+    new,
+    props, classes, owners, locals_, density, rest, blocks, packed, recv, dense, deposit, edges, halo,
+    load_sem, ready, send_sem, recv_sem, edge_sem, halo_sem,
 ):
+    loads = [
+        pltpu.make_async_copy(src, dst, load_sem.at[i])
+        for i, (src, dst) in enumerate(
+            [(owners_h, owners), (props_h, props), (classes_h, classes), (locals_h, locals_), (density_h, density), (rest_h, rest)]
+        )
+    ]
+    for load in loads:
+        load.start()
     at = here()
     gx, gy = lax.axis_index("gx"), lax.axis_index("gy")
     barrier = pltpu.get_barrier_semaphore()
-    row, column = in_row(at), in_column(at)
-    for to in row + column:
+    plane = in_plane(at)
+    column = [peer(at, 0, dz, 0, 0) for dz in range(1, Z)]
+    for to in column + plane:
         signal(barrier, to)
 
-    pack(props, classes, owners, locals_, table, blocks, packed)
-
-    pl.semaphore_wait(barrier, len(row) + len(column))
-    for to in row:
-        signal(second, to)
-    pl.semaphore_wait(second, len(row))
-
-    order = offsets()
-    for slot, off in enumerate(order):
-        if slot:
-            to = peer(at, *off)
+    for load in loads:
+        load.wait()
+
+    def midway():
+        pl.semaphore_wait(barrier, len(plane) + len(column))
+        for dz in range(1, Z):
+            signal(ready.at[dz], column[dz - 1])
+
+    pack(props, classes, owners, locals_, table, blocks, packed, midway)
+
+    for slot, off in enumerate(offsets()):
+        to = peer(at, *off)
+        if slot % GROUP == 0 and off[1]:
+            pl.semaphore_wait(ready.at[Z - off[1]], 1)
+        if off == (0, 0, 0, 0):
+            recv[slot] = blocks[gx * 8 + gy]
+        else:
             pltpu.make_async_remote_copy(
                 src_ref=blocks.at[to[0] * 8 + to[1]],
                 dst_ref=recv.at[slot],
@@ -212,7 +223,6 @@
                 device_id=to,
                 device_id_type=MESH,
             ).start()
-    recv[0] = blocks[gx * 8 + gy]
 
     def gas_rows(k, h):
         return density[h : h + 1] if k == 0 else rest[k - 1, h : h + 1]
@@ -221,8 +231,11 @@
         pltpu.make_async_copy(blocks.at[:copies], recv.at[:copies], sem).wait()
 
     for group in range(GROUPS):
-        arrived(GROUP if group else GROUP - 1, recv_sem.at[group])
-        receive_group(group, recv, gas_rows, table_s, dense, deposit)
+        arrived(GROUP if PLANES[group] else GROUP - 1, recv_sem.at[group])
+        if group:
+            add_sources(group - 1, dense.at[(group - 1) % 2], deposit)
+        find_sources(group, recv, gas_rows, table_s, dense.at[group % 2])
+    add_sources(GROUPS - 1, dense.at[(GROUPS - 1) % 2], deposit)
     arrived(DEVICES - 1, send_sem)
 
     lane = iota((8, 128), 1)
@@ -277,32 +290,46 @@
             lefts.append(jnp.where(lane == 0, pltpu.roll(left, 128 - i, 1) if i else left, pltpu.roll(tile, 1, 1)))
         around = up + down + jnp.concatenate(rights, axis=0) + jnp.concatenate(lefts, axis=0)
         smooth = 0.4 * field + 0.15 * around
-        if k == 0:
-            new_density[...] = density[...] + smooth
-        else:
-            new_rest[k - 1] = rest[k - 1] + smooth
+        gas = density[...] if k == 0 else rest[k - 1]
+        new[k] = gas + smooth
+
+
+def put_out(new, new_density, new_rest, sem):
+    copies = [
+        pltpu.make_async_copy(new.at[0], new_density, sem.at[0]),
+        pltpu.make_async_copy(new.at[1:], new_rest, sem.at[1]),
+    ]
+    for copy in copies:
+        copy.start()
+    for copy in copies:
+        copy.wait()
 
 
 def per_device(parcel_props, size_class, dest_owner, dest_local, class_table, gas_density, gas_rest):
     vmem = pl.BlockSpec(memory_space=pltpu.VMEM)
+    hbm = pl.BlockSpec(memory_space=pltpu.HBM)
     smem = pl.BlockSpec(memory_space=pltpu.SMEM)
-    return pl.pallas_call(
+    new = pl.pallas_call(
         kernel,
-        out_shape=(
-            jax.ShapeDtypeStruct((LX, LY), F32),
-            jax.ShapeDtypeStruct((4, LX, LY), F32),
-        ),
-        in_specs=[vmem, vmem, vmem, vmem, vmem, smem, vmem, vmem],
-        out_specs=(vmem, vmem),
+        out_shape=jax.ShapeDtypeStruct((5, LX, LY), F32),
+        in_specs=[hbm, hbm, hbm, hbm, vmem, smem, hbm, hbm],
+        out_specs=vmem,
         scratch_shapes=[
+            pltpu.VMEM((16, PARCELS), F32),
+            pltpu.VMEM((32, 128), jnp.int32),
+            pltpu.VMEM((32, 128), jnp.int32),
+            pltpu.VMEM((32, 128), jnp.int32),
+            pltpu.VMEM((LX, LY), F32),
+            pltpu.VMEM((4, LX, LY), F32),
             pltpu.VMEM((DEVICES, WORDS // 2, 128), F32),
             pltpu.VMEM((WORDS * CAP, DEVICES), F32),
             pltpu.VMEM((DEVICES, WORDS // 2, 128), F32),
-            pltpu.VMEM((12, GROUP // 2, 128), F32),
+            pltpu.VMEM((2, 12, GROUP // 2, 128), F32),
             pltpu.VMEM((160, LY), F32),
             pltpu.VMEM((4, 8, 128), F32),
             pltpu.VMEM((4, 8, 128), F32),
-            pltpu.SemaphoreType.REGULAR,
+            pltpu.SemaphoreType.DMA((6,)),
+            pltpu.SemaphoreType.REGULAR((Z,)),
             pltpu.SemaphoreType.DMA,
             pltpu.SemaphoreType.DMA((GROUPS,)),
             pltpu.SemaphoreType.DMA((4,)),
@@ -319,6 +346,16 @@
         gas_density,
         gas_rest,
     )
+    return pl.pallas_call(
+        put_out,
+        out_shape=(
+            jax.ShapeDtypeStruct((LX, LY), F32),
+            jax.ShapeDtypeStruct((4, LX, LY), F32),
+        ),
+        in_specs=[vmem],
+        out_specs=(hbm, hbm),
+        scratch_shapes=[pltpu.SemaphoreType.DMA((2,))],
+    )(new)
 
 
 def solution(mesh):

time: 41 us -> 39.9 us (0.973)
  local copies, waits for them, and re-layouts: 2.8 us -> 0 us
  Pallas kernels: 37.4 us -> 39 us
    unnamed x2 -> x0, local copies, waits for them, and re-layouts: 2.8 us -> none
    pallas_call x1 -> x2, Pallas kernels: 37.4 us -> 39 us  [the longest x1 37.5 us: per_device(): pl.pallas_call(kernel, out_shape=jax.ShapeDtypeStruct((5, LX, LY), F32),...]
where the time goes in v1:
time: 39.9 us; the launch traced here: 39.7 us
  Pallas kernels  39 us (98%)
  between operations  0.64 us (2%)
    pallas_call x1, Pallas kernels, per_device(): pl.pallas_call(kernel, out_shape=jax.ShapeDtypeStruct((5, LX, LY), F32),...  37.5 us
    pallas_call x1, Pallas kernels, per_device(): pl.pallas_call(put_out, out_shape=(jax.ShapeDtypeStruct((LX, LY), F32), j...  1.54 us

profile of v1, /device:TPU:1, one launch (start us, length us, event | category | flops | bytes accessed | tf_op | source)
XLA Modules:
  0.0 39.7 jit_solution(16401764605581303891)
XLA Ops:
  0.6 37.5 %shard_map.86.new = f32[5,32,128]{2,1,0:T(8,128)} custom-call(f32[16,4096]{1,0:T(8,128)} %props_h.1, s32[32,128]{1,0:T(8,128)} %bitcast.3, s32[32,128]{1,0:T(8,128)} %bitcast.4, s32[32,128]{1,0:T(8,128)} %bitcast.5, f32[8,16]{1,0:T(8,128)} %table_s.1, f32[8,16]{1,0:T(8,128)} %table_s.1, f32[32,128]{1,0:T(8,128)} %density_h.1, f32[4,32,128]{2,1,0:T(8,128)} %rest_h.1), custom_call_target="tpu_custom_call" | custom-call | tf_op jit(solution)/shard_map/pallas_call | solution.py:312
  38.1 1.5 %shard_map.87 = (f32[32,128]{1,0:T(8,128)}, f32[4,32,128]{2,1,0:T(8,128)}) custom-call(f32[5,32,128]{2,1,0:T(8,128)} %shard_map.86.new), custom_call_target="tpu_custom_call" | custom-call | tf_op jit(solution)/shard_map/pallas_call | solution.py:349

commit v2 on v1

--- a/solution.py
+++ b/solution.py
@@ -24,7 +24,7 @@
 
 
 def offsets():
-    flat = [(dx, dy, dc) for dx in range(X) for dy in range(Y) for dc in range(CORES)]
+    flat = [(dx, dy, dc) for dx in (2, 1, 3, 0) for dy in (2, 1, 3, 0) for dc in range(CORES)]
     return [(dx, dz, dy, dc) for dz in PLANES for dx, dy, dc in flat]
 
 

time: 39.9 us -> 39.1 us (0.980)
  Pallas kernels: 39 us -> 38.2 us
    pallas_call x1, Pallas kernels: 37.5 us -> 36.6 us  [per_device(): pl.pallas_call(kernel, out_shape=jax.ShapeDtypeStruct((5, LX, LY), F32),...]
where the time goes in v2:
time: 39.1 us; the launch traced here: 38.8 us
  Pallas kernels  38.2 us (98%)
  between operations  0.64 us (2%)
    pallas_call x1, Pallas kernels, per_device(): pl.pallas_call(kernel, out_shape=jax.ShapeDtypeStruct((5, LX, LY), F32),...  36.6 us
    pallas_call x1, Pallas kernels, per_device(): pl.pallas_call(put_out, out_shape=(jax.ShapeDtypeStruct((LX, LY), F32), j...  1.54 us

profile of v2, /device:TPU:1, one launch (start us, length us, event | category | flops | bytes accessed | tf_op | source)
XLA Modules:
  0.0 38.8 jit_solution(11825812715444287900)
XLA Ops:
  0.6 36.6 %shard_map.86.new = f32[5,32,128]{2,1,0:T(8,128)} custom-call(f32[16,4096]{1,0:T(8,128)} %props_h.1, s32[32,128]{1,0:T(8,128)} %bitcast.3, s32[32,128]{1,0:T(8,128)} %bitcast.4, s32[32,128]{1,0:T(8,128)} %bitcast.5, f32[8,16]{1,0:T(8,128)} %table_s.1, f32[8,16]{1,0:T(8,128)} %table_s.1, f32[32,128]{1,0:T(8,128)} %density_h.1, f32[4,32,128]{2,1,0:T(8,128)} %rest_h.1), custom_call_target="tpu_custom_call" | custom-call | tf_op jit(solution)/shard_map/pallas_call | solution.py:312
  37.3 1.5 %shard_map.87 = (f32[32,128]{1,0:T(8,128)}, f32[4,32,128]{2,1,0:T(8,128)}) custom-call(f32[5,32,128]{2,1,0:T(8,128)} %shard_map.86.new), custom_call_target="tpu_custom_call" | custom-call | tf_op jit(solution)/shard_map/pallas_call | solution.py:349
